TPU v7x, 256 devices: a 8x8x2 block of a 8x8x16 slice. The times are simulated.
256 devices in a mesh: groups: 2 (over z), ep: 128 (over y, x, core).
Axes of the slice: x: 8, y: 8, z: 2, core: 2. Of those that a mesh axis runs over, the one named last changes fastest.
The devices are a block of a 8x8x16 slice.
Arguments:
- tokens: bfloat16 [2048, 7168], P(('groups', 'ep')), parts along dimension 0, may hold values from -6 to 6
- experts: int32 [2048, 8], P(('groups', 'ep')), parts along dimension 0, may hold values from 0 to 15, as said below
- gate_fixed: int32 [2048, 8], P(('groups', 'ep')), parts along dimension 0, may hold values from 1 to 65535
- home_slot: int32 [2048], P(('groups', 'ep')), parts along dimension 0, may hold values from 0 to 7, as said below
- bias: float32 [16], replicated, may hold values from -0.5 to 0.5
- w_gate: bfloat16 [7168, 32768], P(None, 'ep'), may hold values from -0.0625 to 0.0625
- w_up: bfloat16 [7168, 32768], P(None, 'ep'), may hold values from -0.0625 to 0.0625
- w_down: bfloat16 [32768, 7168], P('ep'), may hold values from -0.125 to 0.125
Outputs:
- moe_out: bfloat16 [2048, 7168], P(('groups', 'ep')), parts along dimension 0
- bias_next: float32 [32], P('groups'), parts along dimension 0
There are 2 independent parts, one for each index of `groups`. A program takes and returns all parts, laid end to end along the dimension named above; an argument that names none is the same for every part. Nothing has to cross between parts.
Inputs may be any that keep to these rules, and one draw needn't show every extreme that they name: Each token names 8 different experts; among the tokens of one device no expert is named more than 6 times, and some device reaches that bound. `home_slot`: within each device's block of 8 tokens every value appears exactly once.
All inputs are finite; a program needn't handle non-finite values.
Results may differ from a plain program's by a relative error of at most 0.008.
Values may be sent and summed in bfloat16 or wider, within the bound.
A program may use at most 128 MiB of HBM per device.

v0:
```python
import math
import jax
import jax.numpy as jnp
from jax import lax
from jax.sharding import PartitionSpec as P

ROUTED_SCALE = 2.5


def per_device(tokens, experts, gate_fixed, home_slot, bias, w_gate, w_up, w_down):
    tok_rows, width = tokens.shape
    top_count = experts.shape[1]
    expert_count = bias.shape[0]
    device_count = lax.axis_size("ep")
    shards = device_count // expert_count
    meta = jnp.concatenate([experts, gate_fixed // 256, gate_fixed % 256], axis=1)
    rows = jnp.concatenate([tokens, meta.astype(jnp.bfloat16)], axis=1)
    placer = (home_slot[None, :] == jnp.arange(tok_rows, dtype=jnp.int32)[:, None]).astype(
        jnp.bfloat16
    )
    rows = jnp.dot(placer, rows, preferred_element_type=jnp.float32).astype(jnp.bfloat16)
    everyone = lax.all_gather(rows, "ep", axis=0, tiled=True)
    x = everyone[:, :width]
    meta = everyone[:, width:].astype(jnp.float32)
    ids, high, low = (
        meta[:, :top_count],
        meta[:, top_count : 2 * top_count],
        meta[:, 2 * top_count :],
    )
    fixed = high * 256.0 + low
    share = ROUTED_SCALE * fixed / jnp.sum(fixed, axis=1, keepdims=True)
    own = (lax.axis_index("ep") // shards).astype(jnp.float32)
    gate = jnp.sum(jnp.where(ids == own, share, 0.0), axis=1, keepdims=True)
    gate_part = jnp.dot(x, w_gate, preferred_element_type=jnp.float32)
    up_part = jnp.dot(x, w_up, preferred_element_type=jnp.float32)
    hidden = (jax.nn.silu(gate_part) * up_part * gate).astype(jnp.bfloat16)
    part = jnp.dot(hidden, w_down, preferred_element_type=jnp.float32).astype(jnp.bfloat16)
    out = lax.psum_scatter(part, "ep", scatter_dimension=0, tiled=True)
    hits = ids[:, :, None] == jnp.arange(expert_count, dtype=jnp.float32)[None, None, :]
    loads = jnp.sum(hits.astype(jnp.float32), axis=(0, 1))
    average = tok_rows * device_count * top_count / expert_count
    bias_next = bias + 2.0 / math.sqrt(average) * (average - loads)
    return (out, bias_next)


def solution(mesh):
    placed = (
        P(("groups", "ep"), None),
        P(("groups", "ep"), None),
        P(("groups", "ep"), None),
        P(("groups", "ep")),
        P(),
        P(None, "ep"),
        P(None, "ep"),
        P("ep", None),
    )
    return jax.shard_map(
        per_device,
        mesh=mesh,
        in_specs=placed,
        out_specs=(P(("groups", "ep"), None), P("groups")),
        check_vma=False,
    )
```

profile of v0, /device:TPU:516, one launch (start us, length us, event | category | flops | bytes accessed | tf_op | source)
XLA Modules:
  0.0 376.1 jit_solution(18024475353310165763)
XLA Ops:
  7.2 0.1 all-gather.2.cloned.1.call-start
  7.2 0.7 convert.9
  7.9 0.7 fusion.24
  8.6 1.0 concatenate.6
  9.6 1.5 convolution_convert_fusion.1
  11.1 0.1 all-gather.2.cloned.1.call-update
  11.1 0.1 reduce-scatter.2.cloned.1.call-start
  11.2 110.1 %all-gather.2.cloned.1.call-done = bf16[1024,7192]{1,0:T(8,128)(2,1)} async-done(((bf16[8,7192]{1,0:T(8,128)(2,1)}), bf16[1024,7192]{1,0:T(8,128)(2,1)}) %all-gather.2.cloned.1.call-update) | async-done | bytes 14729232 | tf_op jit(solution)/shard_map/all_gather | solution.py:22
  121.3 1.0 slice_convert_fusion
  122.3 0.5 fusion.29
  122.8 0.6 select_reduce_fusion
  123.5 8.3 %fusion.2 = f32[1024,256]{1,0:T(8,128)S(1)} fusion(bf16[7168,256]{1,0:T(8,128)(2,1)} %param.13, bf16[1024,7192]{1,0:T(8,128)(2,1)} %all-gather.2.cloned.1.call-done), kind=kOutput, calls=%fused_computation.3 | convolution fusion | flops 3758096384 | bytes 19398656 | tf_op jit(solution)/shard_map/dot_general | solution.py:34
  131.8 23.7 %convolution_convert_fusion = bf16[1024,7168]{1,0:T(8,128)(2,1)} fusion(bf16[256,7168]{1,0:T(8,128)(2,1)} %param.15, bf16[7168,256]{1,0:T(8,128)(2,1)} %param.14, bf16[1024,7192]{1,0:T(8,128)(2,1)} %all-gather.2.cloned.1.call-done, f32[1024,256]{1,0:T(8,128)S(1)} %fusion.2, f32[1024]{0:T(1024)S(1)} %select_reduce_fusion), kind=kOutput, calls=%fused_computation | convolution fusion | flops 7525367808 | bytes 37752832 | tf_op jit(solution)/shard_map/dot_general | solution.py:37
  155.5 0.0 copy-start
  155.5 0.1 reduce-scatter.2.cloned.1.call-update
  155.5 0.2 copy.10
  155.7 0.2 convert_reduce_fusion
  155.9 0.2 copy-done
  156.1 0.5 multiply_add_fusion
  156.6 212.6 %reduce-scatter.2.cloned.1.call-done = bf16[8,7168]{1,0:T(8,128)(2,1)} async-done(((bf16[1024,7168]{1,0:T(8,128)(2,1)}), bf16[8,7168]{1,0:T(8,128)(2,1)}) %reduce-scatter.2.cloned.1.call-update) | async-done | bytes 114704 | tf_op jit(solution)/shard_map/reduce_scatter | solution.py:38
Async XLA Ops:
  7.2 114.2 %all-gather.2.cloned.1.call-start = ((), (), s32[]{:S(2)}) async-start(), calls=%async_computation.1 | async-start | bytes 15058944 | tf_op jit(solution)/shard_map/all_gather | solution.py:22
  11.1 358.1 %reduce-scatter.2.cloned.1.call-start = ((), (), s32[]{:S(2)}) async-start(), calls=%async_computation.2 | async-start | bytes 14794752 | tf_op jit(solution)/shard_map/reduce_scatter | solution.py:38
  155.5 0.7 copy-start
Sparse Core Ops, SparseCore 0:
  11.3 110.0 all-gather.1
  155.6 213.5 reduce-scatter.1
where the time goes:
time: 376 us
  waiting for transfers between devices  323 us (86%)
  matrix products  33.4 us (9%)
  between operations  14.1 us (4%)
  other arithmetic  4.24 us (1%)
    reduce_scatter x1, waiting for transfers between devices, per_device(): out = lax.psum_scatter(part, 'ep', scatter_dimension=0, tiled=True)  213 us
    all_gather x1, waiting for transfers between devices, per_device(): everyone = lax.all_gather(rows, 'ep', axis=0, tiled=True)  110 us
    dot_general x1, matrix products, per_device(): jnp.dot(hidden, w_down, preferred_element_type=jnp.float32)  23.7 us
    dot_general x1, matrix products, per_device(): gate_part = jnp.dot(x, w_gate, preferred_element_type=jnp.float32)  8.3 us
  transfers between devices with their start and end apart: 2, of which 2 were waited for; matrix products, arithmetic and copies ran while one was open for 0% of the time, Pallas kernels for 0%

commit v1 on v0

--- a/solution.py
+++ b/solution.py
@@ -19,7 +19,9 @@
         jnp.bfloat16
     )
     rows = jnp.dot(placer, rows, preferred_element_type=jnp.float32).astype(jnp.bfloat16)
-    everyone = lax.all_gather(rows, "ep", axis=0, tiled=True)
+    everyone = jnp.concatenate(
+        lax.all_to_all(jnp.stack([rows] * lax.axis_size("ep")), "ep", 0, 0), axis=0
+    )
     x = everyone[:, :width]
     meta = everyone[:, width:].astype(jnp.float32)
     ids, high, low = (

time: 376 us -> 779 us (2.07)
  waiting for transfers between devices: 323 us -> 693 us
  starting transfers between devices: 0.13 us -> 27.5 us
    all_to_all x0 -> x1, waiting for transfers between devices: none -> 474 us  [per_device(): lax.all_to_all(jnp.stack([rows] * lax.axis_size('ep')), 'ep', 0, 0)]
    all_gather x1 -> x0, waiting for transfers between devices: 110 us -> none  [per_device(): everyone = lax.all_gather(rows, 'ep', axis=0, tiled=True)]
    all_to_all x0 -> x1, starting transfers between devices: none -> 27.2 us  [per_device(): lax.all_to_all(jnp.stack([rows] * lax.axis_size('ep')), 'ep', 0, 0)]
where the time goes in v1:
time: 779 us; the launch traced here: 778 us
  waiting for transfers between devices  693 us (89%)
  matrix products  32.8 us (4%)
  starting transfers between devices  27.5 us (4%)
  between operations  14.1 us (2%)
  local copies, waits for them, and re-layouts  8.64 us (1%)
    all_to_all x1, waiting for transfers between devices, per_device(): lax.all_to_all(jnp.stack([rows] * lax.axis_size('ep')), 'ep', 0, 0)  474 us
    reduce_scatter x1, waiting for transfers between devices, per_device(): out = lax.psum_scatter(part, 'ep', scatter_dimension=0, tiled=True)  219 us
    all_to_all x1, starting transfers between devices, per_device(): lax.all_to_all(jnp.stack([rows] * lax.axis_size('ep')), 'ep', 0, 0)  27.2 us
    dot_general x1, matrix products, per_device(): jnp.dot(hidden, w_down, preferred_element_type=jnp.float32)  23.7 us
  transfers between devices with their start and end apart: 2, of which 2 were waited for; matrix products, arithmetic and copies ran while one was open for 0% of the time, Pallas kernels for 0%

profile of v1, /device:TPU:516, one launch (start us, length us, event | category | flops | bytes accessed | tf_op | source)
XLA Modules:
  0.0 778.3 jit_solution(13545535758666934282)
XLA Ops:
  7.2 0.7 convert.9
  7.9 0.7 fusion.24
  8.6 1.0 concatenate.6
  9.6 0.8 convolution_convert_fusion.1
  10.4 6.2 stack.2
  16.6 27.2 %all-to-all-start = ((bf16[128,8,7192]{2,1,0:T(8,128)(2,1)}), bf16[128,8,7192]{2,1,0:T(8,128)(2,1)}, u32[]{:S(2)}, u32[]{:S(2)}) async-start(bf16[128,8,7192]{2,1,0:T(8,128)(2,1)} %stack.2), calls=%async_computation | async-start | bytes 29884416 | tf_op jit(solution)/shard_map/all_to_all | solution.py:23
  43.8 0.2 reduce-scatter.2.cloned.1.call-start
  44.0 473.7 %all-to-all-done = bf16[128,8,7192]{2,1,0:T(8,128)(2,1)} async-done(((bf16[128,8,7192]{2,1,0:T(8,128)(2,1)}), bf16[128,8,7192]{2,1,0:T(8,128)(2,1)}, u32[]{:S(2)}, u32[]{:S(2)}) %all-to-all-start) | async-done | bytes 14729248 | tf_op jit(solution)/shard_map/all_to_all | solution.py:23
  517.8 1.0 slice.21
  518.7 0.1 copy.20
  518.9 8.3 %fusion.2 = f32[1024,256]{1,0:T(8,128)S(1)} fusion(bf16[7168,256]{1,0:T(8,128)(2,1)} %param.13, bf16[1024,7192]{1,0:T(8,128)(2,1)} %bitcast), kind=kOutput, calls=%fused_computation.3 | convolution fusion | flops 3758096384 | bytes 19398656 | tf_op jit(solution)/shard_map/dot_general | solution.py:36
  527.2 23.7 %convolution_convert_fusion = bf16[1024,7168]{1,0:T(8,128)(2,1)} fusion(bf16[256,7168]{1,0:T(8,128)(2,1)} %param.15, bf16[7168,256]{1,0:T(8,128)(2,1)} %param.14, bf16[1024,7192]{1,0:T(8,128)(2,1)} %bitcast, f32[1024,256]{1,0:T(8,128)S(1)} %fusion.2, f32[1024]{0:T(1024)S(1)} %select_reduce_fusion), kind=kOutput, calls=%fused_computation | convolution fusion | flops 7525367808 | bytes 37752832 | tf_op jit(solution)/shard_map/dot_general | solution.py:39
  550.9 0.0 copy-start
  550.9 0.1 reduce-scatter.2.cloned.1.call-update
  551.0 0.2 convert_reduce_fusion
  551.2 0.4 copy-done
  551.5 0.5 multiply_add_fusion
  552.1 219.4 %reduce-scatter.2.cloned.1.call-done = bf16[8,7168]{1,0:T(8,128)(2,1)} async-done(((bf16[1024,7168]{1,0:T(8,128)(2,1)}), bf16[8,7168]{1,0:T(8,128)(2,1)}) %reduce-scatter.2.cloned.1.call-update) | async-done | bytes 114704 | tf_op jit(solution)/shard_map/reduce_scatter | solution.py:40
  (4 shorter events, 0.1 us)
Async XLA Ops:
  16.6 501.2 %all-to-all-start = ((bf16[128,8,7192]{2,1,0:T(8,128)(2,1)}), bf16[128,8,7192]{2,1,0:T(8,128)(2,1)}, u32[]{:S(2)}, u32[]{:S(2)}) async-start(bf16[128,8,7192]{2,1,0:T(8,128)(2,1)} %stack.2), calls=%async_computation | async-start | bytes 29884416 | tf_op jit(solution)/shard_map/all_to_all | solution.py:23
  43.8 727.7 %reduce-scatter.2.cloned.1.call-start = ((), (), s32[]{:S(2)}) async-start(), calls=%async_computation.2 | async-start | bytes 14794752 | tf_op jit(solution)/shard_map/reduce_scatter | solution.py:40
  550.9 0.7 copy-start
Sparse Core Ops, SparseCore 0:
  551.1 220.3 reduce-scatter.1
